TPU v7x, 256 devices: a whole 4x4x8 slice. The times are simulated.
256 devices in a mesh: vox: 32 (over x, z), frm: 8 (over y, core).
Axes of the slice: x: 4, y: 4, z: 8, core: 2. Of those that a mesh axis runs over, the one named last changes fastest.
Arguments:
- casorati: float32 [256, 1048576], P('frm', 'vox'), may hold values from -6 to 6
- start_vectors: float32 [256, 64], replicated, may hold values from -6 to 6
Outputs:
- vectors: float32 [256, 64], replicated
- filtered: float32 [256, 1048576], P('frm', 'vox')
All inputs are finite; a program needn't handle non-finite values.
Results may differ from a plain program's by a relative error of at most 0.0003.
Values sent between devices are 32-bit elements; how exact they have to be, the bound alone decides.
A program may use at most 64 MiB of HBM per device.

v0:
```python
import jax
import jax.numpy as jnp
from jax import lax
from jax.sharding import PartitionSpec as P

ITERS = 3


def orthonormal(projected):
    small = jnp.dot(projected.T, projected, precision=lax.Precision.HIGHEST)
    lower = jnp.linalg.cholesky(small)
    return jax.scipy.linalg.solve_triangular(lower, projected.T, lower=True).T


def contract_cols(left, right):
    return lax.dot_general(left, right, (((1,), (1,)), ((), ())), precision=lax.Precision.HIGHEST)


def body(casorati, start_vectors):
    high = lax.Precision.HIGHEST
    columns = lax.all_to_all(casorati, "frm", split_axis=1, concat_axis=0, tiled=True)
    vectors = start_vectors
    gram = lax.psum(contract_cols(columns, columns), ("vox", "frm"))
    for step in range(ITERS):
        vectors = orthonormal(jnp.dot(gram, vectors, precision=high))
    image = jnp.dot(vectors.T, columns, precision=high)
    cleaned = columns - jnp.dot(vectors, image, precision=high)
    filtered = lax.all_to_all(cleaned, "frm", split_axis=0, concat_axis=1, tiled=True)
    return (vectors, filtered)


def solution(mesh):
    return jax.shard_map(
        body,
        mesh=mesh,
        in_specs=(P("frm", "vox"), P()),
        out_specs=(P(), P("frm", "vox")),
        check_vma=False,
    )
```

profile of v0, /device:TPU:1, one launch (start us, length us, event | category | flops | bytes accessed | tf_op | source)
XLA Modules:
  0.0 439.2 jit_solution(6300421162435829649)
XLA Ops:
  7.2 0.0 copy-start
  7.2 0.0 all-reduce.2.cloned.1.call-start
  7.2 2.5 copy.12
  9.7 54.4 %all_to_all.38 = f32[32,8,4096]{2,0,1:T(8,128)S(1)} all-to-all(f32[32,8,4096]{2,0,1:T(8,128)S(1)} %bitcast.71), channel_id=1, replica_groups=mesh['vox'=32,'frm'=8] {'frm'}, dimensions={1} | all-to-all | bytes 8388608 | tf_op jit(solution)/shard_map/all_to_all | solution.py:21
  64.1 0.0 copy-start.1
  64.1 2.0 copy-done.1
  66.1 4.2 fusion.19
  70.4 0.0 all-reduce.2.cloned.1.call-update
  70.4 254.1 %all-reduce.2.cloned.1.call-done = f32[256,256]{1,0:T(8,128)} async-done(((f32[256,256]{1,0:T(8,128)}), f32[256,256]{1,0:T(8,128)}) %all-reduce.2.cloned.1.call-update) | async-done | bytes 262160 | tf_op jit(solution)/shard_map/psum | solution.py:23
  324.5 0.0 copy-done
  324.5 1.3 fusion.20
  325.8 0.2 fusion.21
  326.0 0.1 copy.5
  326.1 5.8 %cholesky.59 = f32[64,64]{1,0:T(8,128)S(1)} custom-call(f32[64,64]{1,0:T(8,128)S(1)} %fusion.14), custom_call_target="Cholesky" | custom-call | tf_op jit(solution)/shard_map/jit(cholesky)/cholesky | solution.py:11
  332.0 0.6 compare_reduce_fusion.2
  332.7 0.7 fusion.6
  333.3 4.9 %custom-call.7 = f32[1,64,64]{1,2,0:T(8,128)S(1)} custom-call(f32[1,64,64]{2,1,0:T(8,128)S(1)} %fusion.6), custom_call_target="InvertDiagBlocksLowerTriangular" | custom-call | tf_op jit(solution)/shard_map/jit(_solve_triangular)/triangular_solve | solution.py:12
  338.2 0.3 fusion.4
  338.5 1.3 fusion.22
  339.8 0.2 fusion.23
  340.0 0.1 copy.6
  340.1 5.8 %cholesky.70 = f32[64,64]{1,0:T(8,128)S(1)} custom-call(f32[64,64]{1,0:T(8,128)S(1)} %fusion.12), custom_call_target="Cholesky" | custom-call | tf_op jit(solution)/shard_map/jit(cholesky)/cholesky | solution.py:11
  346.0 0.6 compare_reduce_fusion.1
  346.7 0.7 fusion.7
  347.3 4.9 %custom-call.8 = f32[1,64,64]{1,2,0:T(8,128)S(1)} custom-call(f32[1,64,64]{2,1,0:T(8,128)S(1)} %fusion.7), custom_call_target="InvertDiagBlocksLowerTriangular" | custom-call | tf_op jit(solution)/shard_map/jit(_solve_triangular)/triangular_solve | solution.py:12
  352.2 0.3 fusion.2
  352.5 1.3 fusion.24
  353.8 0.2 fusion.25
  354.0 0.1 copy.7
  354.1 5.8 %cholesky.81 = f32[64,64]{1,0:T(8,128)S(1)} custom-call(f32[64,64]{1,0:T(8,128)S(1)} %fusion.10), custom_call_target="Cholesky" | custom-call | tf_op jit(solution)/shard_map/jit(cholesky)/cholesky | solution.py:11
  360.0 0.6 compare_reduce_fusion
  360.6 0.7 fusion.8
  361.3 4.9 %custom-call.9 = f32[1,64,64]{1,2,0:T(8,128)S(1)} custom-call(f32[1,64,64]{2,1,0:T(8,128)S(1)} %fusion.8), custom_call_target="InvertDiagBlocksLowerTriangular" | custom-call | tf_op jit(solution)/shard_map/jit(_solve_triangular)/triangular_solve | solution.py:12
  366.2 0.0 copy-start.2
  366.2 0.3 fusion
  366.5 0.0 copy-start.3
  366.5 5.2 %fusion.26 = f32[64,4096]{1,0:T(8,128)S(1)} fusion(f32[64,256]{1,0:T(8,128)S(1)} %fusion, f32[256,4096]{1,0:T(8,128)} %bitcast.67), kind=kOutput, calls=%fused_computation.40 | convolution fusion | flops 805306368 | bytes 5308416 | tf_op jit(solution)/shard_map/dot_general | solution.py:26
  371.7 0.0 copy-done.2
  371.7 3.5 convolution_subtract_fusion
  375.2 0.0 copy-done.3
  375.2 54.9 %all_to_all.39 = f32[8,32,4096]{2,1,0:T(8,128)S(1)} all-to-all(f32[8,32,4096]{2,1,0:T(8,128)S(1)} %bitcast.69), channel_id=1, replica_groups=mesh['vox'=32,'frm'=8] {'frm'}, dimensions={0} | all-to-all | bytes 8388608 | tf_op jit(solution)/shard_map/all_to_all | solution.py:28
  430.1 2.3 copy.10
  (6 shorter events, 0.1 us)
Async XLA Ops:
  7.2 317.3 %copy-start = (f32[256,64]{0,1:T(8,128)S(1)}, f32[256,64]{0,1:T(8,128)}, u32[]{:S(2)}) copy-start(f32[256,64]{0,1:T(8,128)} %param.6) | copy-start | bytes 196612
  7.2 317.3 %all-reduce.2.cloned.1.call-start = ((), (), s32[]{:S(2)}) async-start(), calls=%async_computation.2 | async-start | bytes 524288 | tf_op jit(solution)/shard_map/psum | solution.py:23
  64.1 2.0 copy-start.1
  366.2 5.4 %copy-start.2 = (f32[32,8,4096]{2,0,1:T(8,128)S(1)}, f32[32,8,4096]{2,0,1:T(8,128)}, u32[]{:S(2)}) copy-start(f32[32,8,4096]{2,0,1:T(8,128)} %copy-done.1) | copy-start | bytes 12582916
  366.5 8.7 %copy-start.3 = (f32[64,256]{1,0:T(8,128)}, f32[64,256]{1,0:T(8,128)S(1)}, u32[]{:S(2)}) copy-start(f32[64,256]{1,0:T(8,128)S(1)} %fusion) | copy-start | bytes 196612
Sparse Core Ops, SparseCore 0:
  70.5 253.9 all-reduce.1
where the time goes:
time: 440 us; the launch traced here: 439 us
  waiting for transfers between devices  254 us (58%)
  blocking collectives  109 us (25%)
  other arithmetic  36.2 us (8%)
  matrix products  18.3 us (4%)
  between operations  14.2 us (3%)
  local copies, waits for them, and re-layouts  7.04 us (2%)
    psum x1, waiting for transfers between devices, body(): gram = lax.psum(contract_cols(columns, columns), ('vox', 'frm'))  254 us
    all_to_all x1, blocking collectives, body(): lax.all_to_all(cleaned, 'frm', split_axis=0, concat_axis=1, tiled=True)  54.9 us
    all_to_all x1, blocking collectives, body(): lax.all_to_all(casorati, 'frm', split_axis=1, concat_axis=0, tiled=True)  54.4 us
    another operation x9, other arithmetic, orthonormal(): lower = jnp.linalg.cholesky(small)  19.6 us
    another operation x6, other arithmetic, orthonormal(): return jax.scipy.linalg.solve_triangular(lower, projected.T, lower=True).T  16.6 us
  transfers between devices with their start and end apart: 1, of which 1 were waited for; matrix products, arithmetic and copies ran while one was open for 0% of the time, Pallas kernels for 0%

commit v1 on v0

v1 whole, which is shorter than its diff:
```python
import functools

import jax
import jax.numpy as jnp
from jax import lax
from jax.experimental import pallas as pl
from jax.experimental.pallas import tpu as pltpu
from jax.sharding import PartitionSpec as P

ITERS = 3
MESH = pl.DeviceIdType.MESH
HIGH = lax.Precision.HIGHEST
NY = 4
NX = 4
PARTS = 4
SUBS = 8


def orthonormal(projected):
    small = jnp.dot(projected.T, projected, precision=HIGH)
    lower = jnp.linalg.cholesky(small)
    return jax.scipy.linalg.solve_triangular(lower, projected.T, lower=True).T


def remote(src, dst, send, recv, axis, index):
    return pltpu.make_async_remote_copy(
        src_ref=src, dst_ref=dst, send_sem=send, recv_sem=recv,
        device_id={axis: index}, device_id_type=MESH,
    )


def cut(start, size):
    return pl.ds(pl.multiple_of(start, size), size)


def greet(peers):
    barrier = pltpu.get_barrier_semaphore()
    for axis, index in peers:
        pl.semaphore_signal(barrier, inc=1, device_id={axis: index}, device_id_type=MESH)
    pl.semaphore_wait(barrier, len(peers))


def gram_kernel(nf, nz, c_ref, gram_ref, keep_ref, cols, relay, part, rs, row, xb, zb, fin, full,
                local_sem, keep_sem, hop_send, hop_recv, near_send, near_recv, far_send, far_recv,
                mate_send, mate_recv, f_send, f_recv, x_send, x_recv, z_send, z_recv,
                ax_send, ax_recv, af_send, af_recv):
    me, vox = lax.axis_index("frm"), lax.axis_index("vox")
    y, core = lax.div(me, 2), lax.rem(me, 2)
    x, z = lax.div(vox, nz), lax.rem(vox, nz)
    rows, width = c_ref.shape[0], c_ref.shape[1] // nf
    half = width // 2
    piece = half // PARTS
    nb = (lax.rem(y + 1, NY), lax.rem(y + NY - 1, NY))
    back = (nb[1], nb[0])
    far = lax.rem(y + 2, NY)
    mate = y * 2 + 1 - core

    frm_peers = [("frm", lax.rem(me + r, nf)) for r in range(1, nf)]
    x_peers = [("vox", lax.rem(x + r, NX) * nz + z) for r in range(1, NX)]
    z_peers = [("vox", x * nz + lax.rem(z + r, nz)) for r in range(1, nz)]
    greet(frm_peers + x_peers + z_peers)

    mine = cut(me * rows, rows)
    sends = []
    hops = {}
    for c2 in range(2):
        for d in range(2):
            hops[d, c2] = remote(
                c_ref.at[:, pl.ds(pl.multiple_of((far * 2 + c2) * width + d * half, half), half)],
                relay.at[d, c2], hop_send.at[d, c2], hop_recv.at[d, c2], "frm", nb[d] * 2 + core)
            hops[d, c2].start()
            sends.append(hops[d, c2])
    for c2 in range(2):
        for d in range(2):
            copy = remote(
                c_ref.at[:, cut((nb[d] * 2 + c2) * width, width)], cols.at[mine, :],
                near_send.at[d, c2], near_recv.at[d, core], "frm", nb[d] * 2 + c2)
            copy.start()
            sends.append(copy)
    to_mate = remote(c_ref.at[:, cut(mate * width, width)], cols.at[mine, :], mate_send, mate_recv, "frm", mate)
    to_mate.start()
    sends.append(to_mate)
    local = pltpu.make_async_copy(c_ref.at[:, cut(me * width, width)], cols.at[mine, :], local_sem)
    local.start()

    for c2 in range(2):
        for d in range(2):
            hops[d, c2].wait_recv()
    for s in range(PARTS):
        for c2 in range(2):
            for d in range(2):
                origin = back[d] * 2 + core
                copy = remote(
                    relay.at[d, c2, :, pl.ds(s * piece, piece)],
                    cols.at[cut(origin * rows, rows), pl.ds(d * half + s * piece, piece)],
                    far_send.at[s, d, c2], far_recv.at[s, d, core], "frm", nb[d] * 2 + c2)
                copy.start()
                sends.append(copy)

    local.wait()
    from_mate = remote(
        c_ref.at[:, cut(mate * width, width)], cols.at[cut(mate * rows, rows), :], mate_send, mate_recv, "frm", mate)
    from_mate.wait_recv()
    for d in range(2):
        for c2 in range(2):
            origin = back[d] * 2 + c2
            remote(
                c_ref.at[:, cut(origin * width, width)], cols.at[cut(origin * rows, rows), :],
                near_send.at[d, c2], near_recv.at[d, c2], "frm", origin).wait_recv()

    part[...] = jnp.zeros_like(part)

    def gather(t, carry):
        s, d = lax.div(t, 2), lax.rem(t, 2)
        at = pl.multiple_of(d * half + s * piece, piece)
        for c2 in range(2):
            origin = far * 2 + c2
            remote(
                relay.at[d, c2, :, pl.ds(pl.multiple_of(s * piece, piece), piece)],
                cols.at[cut(origin * rows, rows), pl.ds(at, piece)],
                far_send.at[s, d, c2], far_recv.at[s, d, c2], "frm", origin).wait_recv()
        block = cols[:, pl.ds(at, piece)]
        part[...] += lax.dot_general(
            block, block, (((1,), (1,)), ((), ())), precision=HIGH, preferred_element_type=jnp.float32)
        return carry

    lax.fori_loop(0, 2 * PARTS, gather, 0)
    keep = pltpu.make_async_copy(cols, keep_ref, keep_sem)
    keep.start()

    copies = []
    for r in range(1, nf):
        peer = lax.rem(me + r, nf)
        copies.append(remote(part.at[cut(peer * rows, rows), :], rs.at[me], f_send.at[r], f_recv.at[r], "frm", peer))
        copies[-1].start()
    rs[me] = part[mine, :]
    for copy in copies:
        copy.wait_recv()
    sends += copies
    row[...] = functools.reduce(jnp.add, [rs[k] for k in range(nf)])

    eighth = rows // NX
    slot = cut(x * eighth, eighth)
    copies = []
    for r in range(1, NX):
        px = lax.rem(x + r, NX)
        copies.append(remote(
            row.at[cut(px * eighth, eighth), :], xb.at[x], x_send.at[r], x_recv.at[r], "vox", px * nz + z))
        copies[-1].start()
    xb[x] = row[slot, :]
    for copy in copies:
        copy.wait_recv()
    sends += copies
    zb[z] = functools.reduce(jnp.add, [xb[k] for k in range(NX)])

    copies = []
    for r in range(1, nz):
        copies.append(remote(
            zb.at[z], zb.at[z], z_send.at[r], z_recv.at[r], "vox", x * nz + lax.rem(z + r, nz)))
        copies[-1].start()
    for copy in copies:
        copy.wait_recv()
    sends += copies
    fin[slot, :] = functools.reduce(jnp.add, [zb[k] for k in range(nz)])

    copies = []
    for r in range(1, NX):
        copies.append(remote(
            fin.at[slot, :], fin.at[slot, :], ax_send.at[r], ax_recv.at[r], "vox", lax.rem(x + r, NX) * nz + z))
        copies[-1].start()
    for copy in copies:
        copy.wait_recv()
    sends += copies

    copies = []
    for r in range(1, nf):
        copies.append(remote(
            fin, full.at[mine, :], af_send.at[r], af_recv.at[r], "frm", lax.rem(me + r, nf)))
        copies[-1].start()
    for copy in sends:
        copy.wait_send()
    gram_ref[mine, :] = fin[...]
    for r in range(1, nf):
        peer = lax.rem(me + nf - r, nf)
        spot = cut(peer * rows, rows)
        remote(fin, full.at[spot, :], af_send.at[r], af_recv.at[r], "frm", peer).wait_recv()
        gram_ref[spot, :] = full[spot, :]
    for copy in copies:
        copy.wait_send()
    keep.wait()


def filter_kernel(nf, c_ref, keep_ref, vec_ref, vect_ref, out_ref, img, own, cols, res,
                  own_sem, cols_sem, out_sem, near_send, near_recv, far_send, far_recv,
                  m_send, m_recv):
    me = lax.axis_index("frm")
    y, core = lax.div(me, 2), lax.rem(me, 2)
    rows, width = c_ref.shape[0], c_ref.shape[1] // nf
    sub = width // SUBS
    nb = (lax.rem(y + 1, NY), lax.rem(y + NY - 1, NY))
    back = (nb[1], nb[0])
    far = lax.rem(y + 2, NY)
    mate = y * 2 + 1 - core
    load_cols = pltpu.make_async_copy(keep_ref, cols, cols_sem)
    load_cols.start()
    load_own = pltpu.make_async_copy(c_ref, own, own_sem)
    load_own.start()
    greet([("frm", nb[0] * 2 + core), ("frm", nb[1] * 2 + core), ("frm", mate)])

    chips = (y, back[0], back[1], far)

    def at(chip, side, s):
        return pl.ds(pl.multiple_of((chip * 2 + side) * width + s * sub, sub), sub)

    def near(d, s, chip):
        spot = img.at[:, at(chip, core, s)]
        return remote(spot, spot, near_send.at[d, s], near_recv.at[d, s], "frm", nb[d] * 2 + core)

    def relayed(d, s, chip):
        spot = img.at[:, at(chip, core, s)]
        return remote(spot, spot, far_send.at[s], far_recv.at[s], "frm", nb[d] * 2 + core)

    def across(which, s, side):
        spot = img.at[:, at(chips[which], side, s)]
        return remote(spot, spot, m_send.at[which, s], m_recv.at[which, s], "frm", mate)

    mine = vec_ref[cut(me * rows, rows), :]

    def clean(chip, side, s):
        spot = at(chip, side, s)
        res[:, spot] = own[:, spot] - jnp.dot(mine, img[:, spot], precision=HIGH, preferred_element_type=jnp.float32)
        pltpu.make_async_copy(res.at[:, spot], out_ref.at[:, spot], out_sem).start()

    load_cols.wait()

    def first(s, carry):
        img[:, at(y, core, s)] = jnp.dot(
            vect_ref[...], cols[:, cut(s * sub, sub)], precision=HIGH, preferred_element_type=jnp.float32)
        near(0, s, y).start()
        near(1, s, y).start()
        across(0, s, core).start()
        return carry

    lax.fori_loop(0, SUBS, first, 0)
    load_own.wait()

    def second(pair, carry):
        for odd in range(2):
            s = pair * 2 + odd
            for d in range(2):
                near(d, s, back[d]).wait_recv()
                across(1 + d, s, core).start()
                if d == odd:
                    relayed(d, s, back[d]).start()
            clean(y, core, s)
            clean(back[0], core, s)
            clean(back[1], core, s)
            for which in range(3):
                across(which, s, 1 - core).wait_recv()
                clean(chips[which], 1 - core, s)
        return carry

    lax.fori_loop(0, SUBS // 2, second, 0)

    def third(pair, carry):
        for odd in range(2):
            s = pair * 2 + odd
            relayed(odd, s, far).wait_recv()
            across(3, s, core).start()
            clean(far, core, s)
            across(3, s, 1 - core).wait_recv()
            clean(far, 1 - core, s)
        return carry

    lax.fori_loop(0, SUBS // 2, third, 0)

    def last(pair, carry):
        for odd in range(2):
            s = pair * 2 + odd
            for d in range(2):
                near(d, s, y).wait_send()
            relayed(odd, s, back[odd]).wait_send()
            for which in range(4):
                across(which, s, core).wait_send()
        return carry

    lax.fori_loop(0, SUBS // 2, last, 0)
    pltpu.make_async_copy(res, out_ref, out_sem).wait()


def body(nf, nz, casorati, start_vectors):
    rows, wide = casorati.shape
    frames = rows * nf
    width = wide // nf
    dma = pltpu.SemaphoreType.DMA
    f32 = jnp.float32
    vmem = pl.BlockSpec(memory_space=pltpu.VMEM)
    hbm = pl.BlockSpec(memory_space=pl.ANY)
    eighth = rows // NX
    gram, columns = pl.pallas_call(
        functools.partial(gram_kernel, nf, nz),
        name="gram",
        out_shape=(jax.ShapeDtypeStruct((frames, frames), f32), jax.ShapeDtypeStruct((frames, width), f32)),
        in_specs=[hbm],
        out_specs=(vmem, hbm),
        scratch_shapes=[
            pltpu.VMEM((frames, width), f32),
            pltpu.VMEM((2, 2, rows, width // 2), f32),
            pltpu.VMEM((frames, frames), f32),
            pltpu.VMEM((nf, rows, frames), f32),
            pltpu.VMEM((rows, frames), f32),
            pltpu.VMEM((NX, eighth, frames), f32),
            pltpu.VMEM((nz, eighth, frames), f32),
            pltpu.VMEM((rows, frames), f32),
            pltpu.VMEM((frames, frames), f32),
            dma, dma, dma((2, 2)), dma((2, 2)), dma((2, 2)), dma((2, 2)),
            dma((PARTS, 2, 2)), dma((PARTS, 2, 2)), dma, dma,
            dma((nf,)), dma((nf,)), dma((NX,)), dma((NX,)), dma((nz,)), dma((nz,)),
            dma((NX,)), dma((NX,)), dma((nf,)), dma((nf,)),
        ],
        compiler_params=pltpu.CompilerParams(collective_id=0, has_side_effects=True, vmem_limit_bytes=32 << 20),
    )(casorati)
    vectors = start_vectors
    for step in range(ITERS):
        vectors = orthonormal(jnp.dot(gram, vectors, precision=HIGH))
    filtered = pl.pallas_call(
        functools.partial(filter_kernel, nf),
        name="clean",
        out_shape=jax.ShapeDtypeStruct((rows, wide), f32),
        in_specs=[hbm, hbm, vmem, vmem],
        out_specs=hbm,
        scratch_shapes=[
            pltpu.VMEM((vectors.shape[1], wide), f32),
            pltpu.VMEM((rows, wide), f32),
            pltpu.VMEM((frames, width), f32),
            pltpu.VMEM((rows, wide), f32),
            dma, dma, dma, dma((2, SUBS)), dma((2, SUBS)), dma((SUBS,)), dma((SUBS,)),
            dma((4, SUBS)), dma((4, SUBS)),
        ],
        compiler_params=pltpu.CompilerParams(collective_id=1, has_side_effects=True, vmem_limit_bytes=40 << 20),
    )(casorati, columns, vectors, vectors.T)
    return (vectors, filtered)


def solution(mesh):
    nf, nz = mesh.shape["frm"], mesh.shape["vox"] // NX
    return jax.shard_map(
        functools.partial(body, nf, nz),
        mesh=mesh,
        in_specs=(P("frm", "vox"), P()),
        out_specs=(P(), P("frm", "vox")),
        check_vma=False,
    )
```

time: 440 us -> 174 us (0.40)
  waiting for transfers between devices: 254 us -> 0 us
  Pallas kernels: 0 us -> 123 us
  blocking collectives: 109 us -> 0 us
  matrix products: 18.3 us -> 2.54 us
  between operations: 14.2 us -> 0.82 us
    psum x1 -> x0, waiting for transfers between devices: 254 us -> none  [body(): gram = lax.psum(contract_cols(columns, columns), ('vox', 'frm'))]
    pallas_call x0 -> x2, Pallas kernels: none -> 123 us  [the longest x1 80.3 us: body(): pl.pallas_call(functools.partial(gram_kernel, nf, nz), name='gram', out_s...]
    all_to_all x2 -> x0, blocking collectives: 109 us -> none  [the longest x1 54.9 us: body(): lax.all_to_all(cleaned, 'frm', split_axis=0, concat_axis=1, tiled=True)]
    dot_general x9 -> x6, matrix products: 17.5 us -> 1.73 us  [the longest x3 1.11 us: body(): vectors = orthonormal(jnp.dot(gram, vectors, precision=HIGH))]
    unnamed x8 -> x13, local copies, waits for them, and re-layouts: 2.04 us -> 10.6 us
    all_to_all x2 -> x0, local copies, waits for them, and re-layouts: 4.78 us -> none  [the longest x1 2.47 us: body(): lax.all_to_all(casorati, 'frm', split_axis=1, concat_axis=0, tiled=True)]
  transfers between devices with their start and end apart: 1 -> 0, of which waited for: 1 -> 0; matrix products, arithmetic and copies ran while one was open for 0% -> 0% of each run, Pallas kernels for 0% -> 0%
where the time goes in v1:
time: 174 us
  Pallas kernels  123 us (71%)
  other arithmetic  36.2 us (21%)
  local copies, waits for them, and re-layouts  10.9 us (6%)
  matrix products  2.54 us (1%)
    pallas_call x1, Pallas kernels, body(): pl.pallas_call(functools.partial(gram_kernel, nf, nz), name='gram', out_s...  80.3 us
    pallas_call x1, Pallas kernels, body(): pl.pallas_call(functools.partial(filter_kernel, nf), name='clean', out_sh...  42.8 us
    another operation x9, other arithmetic, orthonormal(): lower = jnp.linalg.cholesky(small)  19.6 us
    another operation x6, other arithmetic, orthonormal(): return jax.scipy.linalg.solve_triangular(lower, projected.T, lower=True).T  16.6 us
    unnamed x13, local copies, waits for them, and re-layouts  10.6 us

profile of v1, /device:TPU:1, one launch (start us, length us, event | category | flops | bytes accessed | tf_op | source)
XLA Modules:
  0.0 173.6 jit_solution(118491327815221162)
XLA Ops:
  0.6 0.0 copy-start
  0.6 0.0 copy-start.1
  0.7 2.2 %copy-done.1 = f32[32,32768]{1,0:T(8,128)S(1)} copy-done((f32[32,32768]{1,0:T(8,128)S(1)}, f32[32,32768]{1,0:T(8,128)}, u32[]{:S(2)}) %copy-start.1) | copy-done | bytes 4194328
  2.9 80.3 %gram.1 = (f32[256,256]{1,0:T(8,128)S(1)}, f32[256,4096]{1,0:T(8,128)S(1)}) custom-call(f32[32,32768]{1,0:T(8,128)S(1)} %copy-done.1), custom_call_target="tpu_custom_call" | custom-call | tf_op jit(solution)/shard_map/gram/pallas_call | solution.py:300
  83.1 0.0 copy-start.3
  83.1 2.0 %copy-done.3 = f32[256,4096]{1,0:T(8,128)} copy-done((f32[256,4096]{1,0:T(8,128)}, f32[256,4096]{1,0:T(8,128)S(1)}, u32[]{:S(2)}) %copy-start.3) | copy-done | bytes 4194328
  85.1 0.0 copy-done
  85.2 0.4 fusion.17
  85.5 0.2 fusion.18
  85.7 0.1 copy.4
  85.8 5.8 %cholesky.59 = f32[64,64]{1,0:T(8,128)S(1)} custom-call(f32[64,64]{1,0:T(8,128)S(1)} %fusion.12), custom_call_target="Cholesky" | custom-call | tf_op jit(solution)/shard_map/jit(cholesky)/cholesky | solution.py:21
  91.7 0.6 compare_reduce_fusion.2
  92.4 0.7 fusion.2
  93.0 4.9 %custom-call.7 = f32[1,64,64]{1,2,0:T(8,128)S(1)} custom-call(f32[1,64,64]{2,1,0:T(8,128)S(1)} %fusion.2), custom_call_target="InvertDiagBlocksLowerTriangular" | custom-call | tf_op jit(solution)/shard_map/jit(_solve_triangular)/triangular_solve | solution.py:22
  97.9 0.3 fusion
  98.2 0.4 fusion.19
  98.6 0.2 fusion.20
  98.8 0.1 copy.5
  98.9 5.8 %cholesky.70 = f32[64,64]{1,0:T(8,128)S(1)} custom-call(f32[64,64]{1,0:T(8,128)S(1)} %fusion.10), custom_call_target="Cholesky" | custom-call | tf_op jit(solution)/shard_map/jit(cholesky)/cholesky | solution.py:21
  104.8 0.6 compare_reduce_fusion.1
  105.4 0.7 fusion.3
  106.1 4.9 %custom-call.8 = f32[1,64,64]{1,2,0:T(8,128)S(1)} custom-call(f32[1,64,64]{2,1,0:T(8,128)S(1)} %fusion.3), custom_call_target="InvertDiagBlocksLowerTriangular" | custom-call | tf_op jit(solution)/shard_map/jit(_solve_triangular)/triangular_solve | solution.py:22
  111.0 0.3 fusion.8
  111.2 0.4 fusion.21
  111.6 0.2 fusion.22
  111.8 0.1 copy.6
  111.9 5.8 %cholesky.81 = f32[64,64]{1,0:T(8,128)S(1)} custom-call(f32[64,64]{1,0:T(8,128)S(1)} %fusion.7), custom_call_target="Cholesky" | custom-call | tf_op jit(solution)/shard_map/jit(cholesky)/cholesky | solution.py:21
  117.8 0.6 compare_reduce_fusion
  118.4 0.7 fusion.4
  119.1 4.9 %custom-call.9 = f32[1,64,64]{1,2,0:T(8,128)S(1)} custom-call(f32[1,64,64]{2,1,0:T(8,128)S(1)} %fusion.4), custom_call_target="InvertDiagBlocksLowerTriangular" | custom-call | tf_op jit(solution)/shard_map/jit(_solve_triangular)/triangular_solve | solution.py:22
  124.0 0.3 fusion.5.vect_ref
  124.3 0.0 copy-start.5
  124.3 0.1 copy.7
  124.4 0.0 copy-start.2
  124.4 2.2 %copy-done.2 = f32[32,32768]{1,0:T(8,128)S(1)} copy-done((f32[32,32768]{1,0:T(8,128)S(1)}, f32[32,32768]{1,0:T(8,128)}, u32[]{:S(2)}) %copy-start.2) | copy-done | bytes 4194328
  126.6 0.0 copy-start.4
  126.6 2.2 %copy-done.4 = f32[256,4096]{1,0:T(8,128)S(1)} copy-done((f32[256,4096]{1,0:T(8,128)S(1)}, f32[256,4096]{1,0:T(8,128)}, u32[]{:S(2)}) %copy-start.4) | copy-done | bytes 4194328
  128.8 42.8 %clean.1 = f32[32,32768]{1,0:T(8,128)S(1)} custom-call(f32[32,32768]{1,0:T(8,128)S(1)} %copy-done.2, f32[256,4096]{1,0:T(8,128)S(1)} %copy-done.4, f32[256,64]{1,0:T(8,128)S(1)} %bitcast.47, f32[64,256]{1,0:T(8,128)S(1)} %fusion.5.vect_ref), custom_call_target="tpu_custom_call" | custom-call | tf_op jit(solution)/shard_map/clean/pallas_call | solution.py:326
  171.5 0.0 copy-done.5
  171.6 2.0 %copy.11 = f32[32,32768]{1,0:T(8,128)} copy(f32[32,32768]{1,0:T(8,128)S(1)} %clean.1) | data formatting | bytes 8388608
  (6 shorter events, 0.1 us)
Async XLA Ops:
  0.6 84.5 %copy-start = (f32[256,64]{0,1:T(8,128)S(1)}, f32[256,64]{0,1:T(8,128)}, u32[]{:S(2)}) copy-start(f32[256,64]{0,1:T(8,128)} %param.6) | copy-start | bytes 196612
  0.6 2.2 %copy-start.1 = (f32[32,32768]{1,0:T(8,128)S(1)}, f32[32,32768]{1,0:T(8,128)}, u32[]{:S(2)}) copy-start(f32[32,32768]{1,0:T(8,128)} %c_ref.3) | copy-start | bytes 12582916
  83.1 2.0 %copy-start.3 = (f32[256,4096]{1,0:T(8,128)}, f32[256,4096]{1,0:T(8,128)S(1)}, u32[]{:S(2)}) copy-start(f32[256,4096]{1,0:T(8,128)S(1)} %get-tuple-element.7.keep_ref) | copy-start | bytes 12582916
  124.3 47.3 %copy-start.5 = (f32[64,256]{1,0:T(8,128)}, f32[64,256]{1,0:T(8,128)S(1)}, u32[]{:S(2)}) copy-start(f32[64,256]{1,0:T(8,128)S(1)} %fusion.5.vect_ref) | copy-start | bytes 196612
  124.4 2.2 %copy-start.2 = (f32[32,32768]{1,0:T(8,128)S(1)}, f32[32,32768]{1,0:T(8,128)}, u32[]{:S(2)}) copy-start(f32[32,32768]{1,0:T(8,128)} %c_ref.3) | copy-start | bytes 12582916
  126.6 2.2 %copy-start.4 = (f32[256,4096]{1,0:T(8,128)S(1)}, f32[256,4096]{1,0:T(8,128)}, u32[]{:S(2)}) copy-start(f32[256,4096]{1,0:T(8,128)} %copy-done.3) | copy-start | bytes 12582916

commit v2 on v1

--- a/solution.py
+++ b/solution.py
@@ -16,10 +16,34 @@
 SUBS = 8
 
 
-def orthonormal(projected):
-    small = jnp.dot(projected.T, projected, precision=HIGH)
-    lower = jnp.linalg.cholesky(small)
-    return jax.scipy.linalg.solve_triangular(lower, projected.T, lower=True).T
+def orthonormal(vt, g_ref):
+    count = vt.shape[0] // 8
+    pt = jnp.dot(vt, g_ref[...], precision=HIGH, preferred_element_type=jnp.float32)
+    twice = jnp.concatenate([pt, pt], axis=0)
+    small = lax.dot_general(pt, twice, (((1,), (1,)), ((), ())), precision=HIGH, preferred_element_type=jnp.float32)
+    lanes = 128
+    wide = pt.shape[1] // lanes
+    rows = [[small[8 * i:8 * i + 8, :]] + [pt[8 * i:8 * i + 8, lanes * q:lanes * (q + 1)] for q in range(wide)] for i in range(count)]
+    line = lax.broadcasted_iota(jnp.int32, (8, lanes), 0)
+    for k in range(count):
+        spread = [[jnp.broadcast_to(rows[i][0][:, 8 * k + j:8 * k + j + 1], (8, lanes)) for j in range(8)] for i in range(k, count)]
+        scale = jnp.zeros((8, lanes), jnp.float32)
+        for j in range(8):
+            root = lax.rsqrt(jnp.broadcast_to(spread[0][j][j:j + 1, :], (8, lanes)))
+            scale = jnp.where(line == j, root, scale)
+            low = [s[j] * root for s in spread]
+            for t in range(j + 1, 8):
+                factor = jnp.broadcast_to(low[0][t:t + 1, :], (8, lanes))
+                for i in range(len(spread)):
+                    spread[i][t] = spread[i][t] - low[i] * factor
+            low[0] = jnp.where(line > j, low[0], 0.0)
+            for q in range(wide + 1):
+                pivot = jnp.broadcast_to(rows[k][q][j:j + 1, :], (8, lanes)) * root
+                for i in range(len(spread)):
+                    rows[k + i][q] = rows[k + i][q] - low[i] * pivot
+        for q in range(1, wide + 1):
+            rows[k][q] = rows[k][q] * scale
+    return jnp.concatenate([jnp.concatenate(rows[i][1:], axis=1) for i in range(count)], axis=0)
 
 
 def remote(src, dst, send, recv, axis, index):
@@ -40,10 +64,10 @@
     pl.semaphore_wait(barrier, len(peers))
 
 
-def gram_kernel(nf, nz, c_ref, gram_ref, keep_ref, cols, relay, part, rs, row, xb, zb, fin, full,
-                local_sem, keep_sem, hop_send, hop_recv, near_send, near_recv, far_send, far_recv,
-                mate_send, mate_recv, f_send, f_recv, x_send, x_recv, z_send, z_recv,
-                ax_send, ax_recv, af_send, af_recv):
+def kernel(nf, nz, c_ref, start_ref, vec_ref, out_ref, cols, relay, part, rs, row, xb, zb, fin, full, vmat, img, own, res,
+           local_sem, own_sem, out_sem, hop_send, hop_recv, near_send, near_recv, far_send, far_recv,
+           mate_send, mate_recv, f_send, f_recv, x_send, x_recv, z_send, z_recv,
+           ax_send, ax_recv, af_send, af_recv, in_send, in_recv, if_send, if_recv, im_send, im_recv):
     me, vox = lax.axis_index("frm"), lax.axis_index("vox")
     y, core = lax.div(me, 2), lax.rem(me, 2)
     x, z = lax.div(vox, nz), lax.rem(vox, nz)
@@ -82,6 +106,8 @@
     sends.append(to_mate)
     local = pltpu.make_async_copy(c_ref.at[:, cut(me * width, width)], cols.at[mine, :], local_sem)
     local.start()
+    load_own = pltpu.make_async_copy(c_ref, own, own_sem)
+    load_own.start()
 
     for c2 in range(2):
         for d in range(2):
@@ -125,8 +151,6 @@
         return carry
 
     lax.fori_loop(0, 2 * PARTS, gather, 0)
-    keep = pltpu.make_async_copy(cols, keep_ref, keep_sem)
-    keep.start()
 
     copies = []
     for r in range(1, nf):
@@ -179,34 +203,24 @@
         copies[-1].start()
     for copy in sends:
         copy.wait_send()
-    gram_ref[mine, :] = fin[...]
+    full[mine, :] = fin[...]
     for r in range(1, nf):
         peer = lax.rem(me + nf - r, nf)
         spot = cut(peer * rows, rows)
         remote(fin, full.at[spot, :], af_send.at[r], af_recv.at[r], "frm", peer).wait_recv()
-        gram_ref[spot, :] = full[spot, :]
     for copy in copies:
         copy.wait_send()
-    keep.wait()
-
-
-def filter_kernel(nf, c_ref, keep_ref, vec_ref, vect_ref, out_ref, img, own, cols, res,
-                  own_sem, cols_sem, out_sem, near_send, near_recv, far_send, far_recv,
-                  m_send, m_recv):
-    me = lax.axis_index("frm")
-    y, core = lax.div(me, 2), lax.rem(me, 2)
-    rows, width = c_ref.shape[0], c_ref.shape[1] // nf
+
+    vec_ref[...] = start_ref[...]
+
+    def turn(step, carry):
+        vec_ref[...] = orthonormal(vec_ref[...], full)
+        return carry
+
+    lax.fori_loop(0, ITERS, turn, 0)
+    vmat[...] = vec_ref[...].T
+
     sub = width // SUBS
-    nb = (lax.rem(y + 1, NY), lax.rem(y + NY - 1, NY))
-    back = (nb[1], nb[0])
-    far = lax.rem(y + 2, NY)
-    mate = y * 2 + 1 - core
-    load_cols = pltpu.make_async_copy(keep_ref, cols, cols_sem)
-    load_cols.start()
-    load_own = pltpu.make_async_copy(c_ref, own, own_sem)
-    load_own.start()
-    greet([("frm", nb[0] * 2 + core), ("frm", nb[1] * 2 + core), ("frm", mate)])
-
     chips = (y, back[0], back[1], far)
 
     def at(chip, side, s):
@@ -214,28 +228,26 @@
 
     def near(d, s, chip):
         spot = img.at[:, at(chip, core, s)]
-        return remote(spot, spot, near_send.at[d, s], near_recv.at[d, s], "frm", nb[d] * 2 + core)
+        return remote(spot, spot, in_send.at[d, s], in_recv.at[d, s], "frm", nb[d] * 2 + core)
 
     def relayed(d, s, chip):
         spot = img.at[:, at(chip, core, s)]
-        return remote(spot, spot, far_send.at[s], far_recv.at[s], "frm", nb[d] * 2 + core)
+        return remote(spot, spot, if_send.at[s], if_recv.at[s], "frm", nb[d] * 2 + core)
 
     def across(which, s, side):
         spot = img.at[:, at(chips[which], side, s)]
-        return remote(spot, spot, m_send.at[which, s], m_recv.at[which, s], "frm", mate)
-
-    mine = vec_ref[cut(me * rows, rows), :]
+        return remote(spot, spot, im_send.at[which, s], im_recv.at[which, s], "frm", mate)
+
+    basis = vmat[mine, :]
 
     def clean(chip, side, s):
         spot = at(chip, side, s)
-        res[:, spot] = own[:, spot] - jnp.dot(mine, img[:, spot], precision=HIGH, preferred_element_type=jnp.float32)
+        res[:, spot] = own[:, spot] - jnp.dot(basis, img[:, spot], precision=HIGH, preferred_element_type=jnp.float32)
         pltpu.make_async_copy(res.at[:, spot], out_ref.at[:, spot], out_sem).start()
-
-    load_cols.wait()
 
     def first(s, carry):
         img[:, at(y, core, s)] = jnp.dot(
-            vect_ref[...], cols[:, cut(s * sub, sub)], precision=HIGH, preferred_element_type=jnp.float32)
+            vec_ref[...], cols[:, cut(s * sub, sub)], precision=HIGH, preferred_element_type=jnp.float32)
         near(0, s, y).start()
         near(1, s, y).start()
         across(0, s, core).start()
@@ -295,13 +307,14 @@
     dma = pltpu.SemaphoreType.DMA
     f32 = jnp.float32
     vmem = pl.BlockSpec(memory_space=pltpu.VMEM)
-    hbm = pl.BlockSpec(memory_space=pl.ANY)
+    hbm = pl.BlockSpec(memory_space=pltpu.HBM)
     eighth = rows // NX
-    gram, columns = pl.pallas_call(
-        functools.partial(gram_kernel, nf, nz),
-        name="gram",
-        out_shape=(jax.ShapeDtypeStruct((frames, frames), f32), jax.ShapeDtypeStruct((frames, width), f32)),
-        in_specs=[hbm],
+    vecs = start_vectors.shape[1]
+    vectors, filtered = pl.pallas_call(
+        functools.partial(kernel, nf, nz),
+        name="clutter",
+        out_shape=(jax.ShapeDtypeStruct((vecs, frames), f32), jax.ShapeDtypeStruct((rows, wide), f32)),
+        in_specs=[hbm, vmem],
         out_specs=(vmem, hbm),
         scratch_shapes=[
             pltpu.VMEM((frames, width), f32),
@@ -313,33 +326,19 @@
             pltpu.VMEM((nz, eighth, frames), f32),
             pltpu.VMEM((rows, frames), f32),
             pltpu.VMEM((frames, frames), f32),
-            dma, dma, dma((2, 2)), dma((2, 2)), dma((2, 2)), dma((2, 2)),
+            pltpu.VMEM((frames, vecs), f32),
+            pltpu.VMEM((vecs, wide), f32),
+            pltpu.VMEM((rows, wide), f32),
+            pltpu.VMEM((rows, wide), f32),
+            dma, dma, dma, dma((2, 2)), dma((2, 2)), dma((2, 2)), dma((2, 2)),
             dma((PARTS, 2, 2)), dma((PARTS, 2, 2)), dma, dma,
             dma((nf,)), dma((nf,)), dma((NX,)), dma((NX,)), dma((nz,)), dma((nz,)),
             dma((NX,)), dma((NX,)), dma((nf,)), dma((nf,)),
+            dma((2, SUBS)), dma((2, SUBS)), dma((SUBS,)), dma((SUBS,)), dma((4, SUBS)), dma((4, SUBS)),
         ],
-        compiler_params=pltpu.CompilerParams(collective_id=0, has_side_effects=True, vmem_limit_bytes=32 << 20),
-    )(casorati)
-    vectors = start_vectors
-    for step in range(ITERS):
-        vectors = orthonormal(jnp.dot(gram, vectors, precision=HIGH))
-    filtered = pl.pallas_call(
-        functools.partial(filter_kernel, nf),
-        name="clean",
-        out_shape=jax.ShapeDtypeStruct((rows, wide), f32),
-        in_specs=[hbm, hbm, vmem, vmem],
-        out_specs=hbm,
-        scratch_shapes=[
-            pltpu.VMEM((vectors.shape[1], wide), f32),
-            pltpu.VMEM((rows, wide), f32),
-            pltpu.VMEM((frames, width), f32),
-            pltpu.VMEM((rows, wide), f32),
-            dma, dma, dma, dma((2, SUBS)), dma((2, SUBS)), dma((SUBS,)), dma((SUBS,)),
-            dma((4, SUBS)), dma((4, SUBS)),
-        ],
-        compiler_params=pltpu.CompilerParams(collective_id=1, has_side_effects=True, vmem_limit_bytes=40 << 20),
-    )(casorati, columns, vectors, vectors.T)
-    return (vectors, filtered)
+        compiler_params=pltpu.CompilerParams(collective_id=0, has_side_effects=True, vmem_limit_bytes=56 << 20),
+    )(casorati, start_vectors.T)
+    return (vectors.T, filtered)
 
 
 def solution(mesh):

time: 174 us -> 135 us (0.78)
  other arithmetic: 36.2 us -> 0 us
  Pallas kernels: 123 us -> 128 us
  local copies, waits for them, and re-layouts: 10.9 us -> 5.94 us
  matrix products: 2.54 us -> 0 us
    another operation x15 -> x0, other arithmetic: 36.2 us -> none  [the longest x9 19.6 us: orthonormal(): lower = jnp.linalg.cholesky(small)]
    pallas_call x2 -> x1, Pallas kernels: 123 us -> 128 us  [body(): pl.pallas_call(functools.partial(kernel, nf, nz), name='clutter', out_sha...]
    unnamed x13 -> x2, local copies, waits for them, and re-layouts: 10.6 us -> 5.94 us
where the time goes in v2:
time: 135 us
  Pallas kernels  128 us (95%)
  local copies, waits for them, and re-layouts  5.94 us (4%)
    pallas_call x1, Pallas kernels, body(): pl.pallas_call(functools.partial(kernel, nf, nz), name='clutter', out_sha...  128 us
    unnamed x2, local copies, waits for them, and re-layouts  5.94 us

profile of v2, /device:TPU:1, one launch (start us, length us, event | category | flops | bytes accessed | tf_op | source)
XLA Modules:
  0.0 134.5 jit_solution(4475269624216557984)
XLA Ops:
  0.6 127.9 %clutter.1 = (f32[64,256]{1,0:T(8,128)}, f32[32,32768]{1,0:T(8,128)}) custom-call(f32[32,32768]{1,0:T(8,128)} %c_ref.1, f32[64,256]{1,0:T(8,128)} %bitcast.2), custom_call_target="tpu_custom_call" | custom-call | tf_op jit(solution)/shard_map/clutter/pallas_call | solution.py:313
  128.6 1.5 %copy.6 = f32[256,64]{0,1:T(8,128)} copy(f32[256,64]{0,1:T(8,128)} %bitcast.3) | data formatting | bytes 131072
  130.0 4.5 %copy.7 = f32[32,32768]{1,0:T(8,128)} copy(f32[32,32768]{1,0:T(8,128)} %get-tuple-element.9) | data formatting | bytes 8388608
